TPU v7x, 256 devices: a whole 4x4x8 slice. The times are simulated.
256 devices in a mesh: mem: 16 (over z, core), ma: 16 (over x, y).
Axes of the slice: x: 4, y: 4, z: 8, core: 2. Of those that a mesh axis runs over, the one named last changes fastest.
Arguments:
- ar_state: float32 [3, 64, 128, 2, 1280], P(None, 'mem', 'ma'), may hold values from -4 to 4
- forcing: float32 [3, 64, 128, 2, 1280], P(None, 'mem', 'ma'), may hold values from -6 to 6
- ar_decay: float32 [3], replicated, may hold values from 0.3 to 0.95
- amplitude: float32 [3, 1280], replicated, may hold values from 0.05 to 0.4
- wavenumber: int32 [128], replicated, may hold values from 0 to 1279, as said below
- tables: bfloat16 [128, 1280, 1280], P('ma', None, 'mem'), may hold values from -0.15625 to 0.15625
- tendencies: bfloat16 [64, 1280, 5120], P('mem', 'ma'), may hold values from -6 to 6
Outputs:
- perturbed: bfloat16 [64, 1280, 5120], P('mem', 'ma')
- new_state: float32 [3, 64, 128, 2, 1280], P(None, 'mem', 'ma')
Inputs may be any that keep to these rules, and one draw needn't show every extreme that they name: `wavenumber`: 128 distinct values.
All inputs are finite; a program needn't handle non-finite values.
Results may differ from a plain program's by a relative error of at most 0.0042.
Values may be sent and summed in bfloat16 or wider, within the bound.
No kernel may reach another device: no remote copies, remote signals or barrier semaphores. Data moves between devices by JAX's collectives and lax.ppermute only.
A program may use at most 64 MiB of HBM per device.

v0:
```python
import math
import jax
import jax.numpy as jnp
from jax import lax
from jax.sharding import PartitionSpec as P

clip_level = 0.9


def basis_table(wavenumber, lon_count):
    longitude = lax.broadcasted_iota(jnp.int32, (wavenumber.shape[0], lon_count), 1)
    phases = wavenumber[:, None] * longitude % lon_count
    angles = phases.astype(jnp.float32) * (2.0 * math.pi / lon_count)
    stacked = jnp.stack([jnp.cos(angles), -jnp.sin(angles)], axis=1)
    return stacked.reshape(2 * wavenumber.shape[0], lon_count).astype(jnp.bfloat16)


def per_device(ar_state, forcing, ar_decay, amplitude, wavenumber, tables, tendencies):
    local_waves = ar_state.shape[2]
    degree_count = ar_state.shape[4]
    owner_index = lax.axis_index("ma")
    own_waves = lax.dynamic_slice_in_dim(wavenumber, owner_index * local_waves, local_waves)
    degree_grid = lax.broadcasted_iota(jnp.int32, (local_waves, degree_count), 1)
    kept_mask = (degree_grid >= own_waves[:, None]).astype(jnp.float32)
    updated = (
        ar_decay[:, None, None, None, None] * ar_state + amplitude[:, None, None, None, :] * forcing
    )
    new_state = kept_mask[None, None, :, None, :] * updated
    coefficients = jnp.sum(new_state, axis=0).astype(jnp.bfloat16)
    everyone = lax.all_gather(coefficients, "mem", axis=0, tiled=True)
    product = jnp.einsum("bmcn,mnl->blmc", everyone, tables, preferred_element_type=jnp.float32)
    fourier = product.astype(jnp.bfloat16)
    banded = lax.all_to_all(
        lax.all_to_all(fourier, "mem", split_axis=0, concat_axis=1, tiled=True),
        "ma",
        split_axis=1,
        concat_axis=2,
        tiled=True,
    )
    member_count, lat_rows, window_size, reim_parts = banded.shape
    basis = basis_table(wavenumber, tendencies.shape[2])
    fourier_rows = banded.reshape(member_count * lat_rows, window_size * reim_parts)
    pattern = jnp.dot(fourier_rows, basis, preferred_element_type=jnp.float32) * (
        1.0 / math.sqrt(window_size)
    )
    pattern = jnp.clip(pattern, -clip_level, clip_level).reshape(tendencies.shape)
    perturbed = (tendencies.astype(jnp.float32) * (1.0 + pattern)).astype(jnp.bfloat16)
    return (perturbed, new_state)


def solution(mesh):
    return jax.shard_map(
        per_device,
        mesh=mesh,
        in_specs=(
            P(None, "mem", "ma", None, None),
            P(None, "mem", "ma", None, None),
            P(),
            P(),
            P(),
            P("ma", None, "mem"),
            P("mem", "ma", None),
        ),
        out_specs=(P("mem", "ma", None), P(None, "mem", "ma", None, None)),
        check_vma=False,
    )
```

profile of v0, /device:TPU:1, one launch (start us, length us, event | category | flops | bytes accessed | tf_op | source)
XLA Modules:
  0.0 131.1 jit_solution(6090136942241296516)
XLA Ops:
  7.2 0.0 copy-start
  7.2 0.0 all-gather.2.cloned.1.call-start
  7.2 0.8 dynamic_slice.3
  8.1 0.1 fusion.20
  8.1 3.5 %fusion.21 = (bf16[4,8,2,1280]{3,2,1,0:T(2,128)(2,1)S(1)}, f32[3,4,8,2,1280]{4,3,2,1,0:T(2,128)}) fusion(f32[3,4,8,2,1280]{4,3,2,1,0:T(2,128)} %param.8, f32[3,1280]{1,0:T(4,128)} %param.10, f32[3,4,8,2,1280]{4,3,2,1,0:T(2,128)} %param.7, f32[3]{0:T(128)} %param.9, f32[8,1280]{1,0:T(8,128)S(1)} %fusion.20), kind=kLoop, calls=%fused_computation.23 | loop fusion | flops 1146880 | bytes 3169292 | tf_op jit(solution)/shard_map/reduce_sum | solution.py:29
  11.6 0.7 copy.23
  12.3 0.0 all-gather.2.cloned.1.call-update
  12.3 0.0 copy-start.2
  12.3 44.4 %all-gather.2.cloned.1.call-done = bf16[64,8,2,1280]{3,1,2,0:T(8,128)(2,1)} async-done(((bf16[4,8,2,1280]{3,1,2,0:T(8,128)(2,1)}), bf16[64,8,2,1280]{3,1,2,0:T(8,128)(2,1)}) %all-gather.2.cloned.1.call-update) | async-done | bytes 2621456 | tf_op jit(solution)/shard_map/all_gather | solution.py:30
  56.7 0.0 copy-done
  56.7 2.7 %fusion.15 = bf16[64,80,8,2]{1,0,3,2:T(8,128)(2,1)S(1)} fusion(bf16[8,1280,80]{1,2,0:T(8,128)(2,1)S(1)} %copy-done, bf16[64,8,2,1280]{3,1,2,0:T(8,128)(2,1)} %all-gather.2.cloned.1.call-done), kind=kOutput, calls=%fused_computation.18 | convolution fusion | flops 209797120 | bytes 4423680 | tf_op jit(solution)/shard_map/bmcn,mnl->blmc/dot_general | solution.py:31
  59.4 1.0 copy.25
  60.4 4.6 %all-to-all-start = ((bf16[64,80,8,2]{1,3,2,0:T(2,128)(2,1)}), bf16[64,80,8,2]{1,3,2,0:T(2,128)(2,1)S(1)}, u32[]{:S(2)}, u32[]{:S(2)}) async-start(bf16[64,80,8,2]{1,3,2,0:T(2,128)(2,1)} %copy.25), calls=%async_computation | async-start | bytes 524288 | tf_op jit(solution)/shard_map/all_to_all | solution.py:34
  65.0 0.0 copy-done.2
  65.0 12.1 %cosine_convert_fusion = (bf16[128,1,5120]{2,0,1:T(8,128)(2,1)S(1)}, bf16[128,1,5120]{2,0,1:T(8,128)(2,1)}) fusion(s32[128]{0:T(128)S(1)} %copy-done.2), kind=kLoop, calls=%fused_computation.11 | loop fusion | flops 7864320 | bytes 2621952 | tf_op jit(solution)/shard_map/convert
  77.1 0.0 all-to-all-done
  77.1 0.2 copy.39
  77.3 4.0 %copy.31 = bf16[4,16,80,8,2]{3,4,0,2,1:T(2,128)(2,1)} copy(bf16[4,16,80,8,2]{2,1,3,4,0:T(8,128)(2,1)S(1)} %bitcast.30) | data formatting | bytes 327680 | tf_op jit(solution)/shard_map/all_to_all | solution.py:34
  81.2 8.6 %reshape.114 = bf16[16,2,2560]{2,1,0:T(2,128)(2,1)} reshape(bf16[1280,4,2,8]{3,2,1,0:T(2,128)(2,1)} %bitcast.26) | data formatting | bytes 327680
  89.8 6.5 %all-to-all-start.1 = ((bf16[16,2,2560]{2,1,0:T(2,128)(2,1)}), bf16[16,2,2560]{2,1,0:T(2,128)(2,1)S(1)}, u32[]{:S(2)}, u32[]{:S(2)}) async-start(bf16[16,2,2560]{2,1,0:T(2,128)(2,1)} %reshape.114), calls=%async_computation.1 | async-start | bytes 327680 | tf_op jit(solution)/shard_map/all_to_all | solution.py:33
  96.4 1.6 %pad_maximum_fusion = bf16[128,2,5120]{2,0,1:T(8,128)(2,1)S(1)} fusion(bf16[128,1,5120]{2,0,1:T(8,128)(2,1)} %get-tuple-element.5, bf16[128,1,5120]{2,0,1:T(8,128)(2,1)S(1)} %get-tuple-element.4), kind=kLoop, calls=%fused_computation.7 | loop fusion | flops 1310720 | bytes 5242880 | tf_op jit(solution)/shard_map/stack | solution.py:14
  97.9 4.2 %copy.29 = bf16[128,2,5120]{2,1,0:T(2,128)(2,1)} copy(bf16[128,2,5120]{2,0,1:T(8,128)(2,1)S(1)} %pad_maximum_fusion) | data formatting | bytes 5242880 | tf_op jit(solution)/shard_map/stack | solution.py:14
  102.1 6.5 %convert_element_type.52 = bf16[256,5120]{1,0:T(8,128)(2,1)} reshape(bf16[128,2,5120]{2,1,0:T(2,128)(2,1)} %copy.29) | data formatting | bytes 5242880 | tf_op jit(solution)/shard_map/convert_element_type | solution.py:15
  108.6 0.0 all-to-all-done.1
  108.6 4.1 %reshape.115 = bf16[1280,4,2,8]{3,2,1,0:T(2,128)(2,1)} reshape(bf16[16,2,2560]{2,1,0:T(2,128)(2,1)S(1)} %all-to-all-done.1) | data formatting | bytes 327680
  112.7 5.2 %copy.28 = bf16[4,16,80,8,2]{2,0,4,3,1:T(4,128)(2,1)S(1)} copy(bf16[4,16,80,8,2]{3,4,0,2,1:T(2,128)(2,1)} %bitcast.27) | data formatting | bytes 327680 | tf_op jit(solution)/shard_map/all_to_all | solution.py:33
  117.9 0.2 reshape.112
  118.1 0.0 copy-start.1
  118.1 3.4 %fusion.1 = f32[320,5120]{1,0:T(8,128)S(1)} fusion(bf16[320,256]{0,1:T(8,128)(2,1)S(1)} %reshape.112, bf16[256,5120]{1,0:T(8,128)(2,1)} %convert_element_type.52), kind=kOutput, calls=%fused_computation.2 | convolution fusion | flops 843776000 | bytes 9338880 | tf_op jit(solution)/shard_map/dot_general | solution.py:43
  121.6 0.0 copy-done.1
  121.6 2.7 %multiply_convert_fusion = bf16[4,80,5120]{2,1,0:T(8,128)(2,1)} fusion(f32[4,80,5120]{2,1,0:T(8,128)S(1)} %bitcast.25, bf16[4,80,5120]{2,1,0:T(8,128)(2,1)S(1)} %copy-done.1), kind=kLoop, calls=%fused_computation.3 | loop fusion | flops 4915200 | bytes 13107200 | tf_op jit(solution)/shard_map/convert_element_type | solution.py:47
Async XLA Ops:
  7.2 49.6 %copy-start = (bf16[8,1280,80]{1,2,0:T(8,128)(2,1)S(1)}, bf16[8,1280,80]{1,2,0:T(8,128)(2,1)}, u32[]{:S(2)}) copy-start(bf16[8,1280,80]{1,2,0:T(8,128)(2,1)} %param.12) | copy-start | bytes 4915204
  7.2 49.6 %all-gather.2.cloned.1.call-start = ((), (), s32[]{:S(2)}) async-start(), calls=%async_computation.2 | async-start | bytes 2785280 | tf_op jit(solution)/shard_map/all_gather | solution.py:30
  12.3 52.7 %copy-start.2 = (s32[128]{0:T(128)S(1)}, s32[128]{0:T(128)}, u32[]{:S(2)}) copy-start(s32[128]{0:T(128)} %param.11) | copy-start | bytes 1540
  60.4 16.7 %all-to-all-start = ((bf16[64,80,8,2]{1,3,2,0:T(2,128)(2,1)}), bf16[64,80,8,2]{1,3,2,0:T(2,128)(2,1)S(1)}, u32[]{:S(2)}, u32[]{:S(2)}) async-start(bf16[64,80,8,2]{1,3,2,0:T(2,128)(2,1)} %copy.25), calls=%async_computation | async-start | bytes 524288 | tf_op jit(solution)/shard_map/all_to_all | solution.py:34
  89.8 18.8 %all-to-all-start.1 = ((bf16[16,2,2560]{2,1,0:T(2,128)(2,1)}), bf16[16,2,2560]{2,1,0:T(2,128)(2,1)S(1)}, u32[]{:S(2)}, u32[]{:S(2)}) async-start(bf16[16,2,2560]{2,1,0:T(2,128)(2,1)} %reshape.114), calls=%async_computation.1 | async-start | bytes 327680 | tf_op jit(solution)/shard_map/all_to_all | solution.py:33
  118.1 3.4 %copy-start.1 = (bf16[4,80,5120]{2,1,0:T(8,128)(2,1)S(1)}, bf16[4,80,5120]{2,1,0:T(8,128)(2,1)}, u32[]{:S(2)}) copy-start(bf16[4,80,5120]{2,1,0:T(8,128)(2,1)} %param.13) | copy-start | bytes 9830404
Sparse Core Ops, SparseCore 0:
  12.4 44.2 all-gather.1
where the time goes:
time: 132 us; the launch traced here: 131 us
  waiting for transfers between devices  44.4 us (34%)
  local copies, waits for them, and re-layouts  35.5 us (27%)
  other arithmetic  19.9 us (15%)
  between operations  14.1 us (11%)
  starting transfers between devices  11.2 us (8%)
  matrix products  6.1 us (5%)
    all_gather x1, waiting for transfers between devices, per_device(): everyone = lax.all_gather(coefficients, 'mem', axis=0, tiled=True)  44.4 us
    unnamed x8, local copies, waits for them, and re-layouts  12.8 us
    another operation x1, other arithmetic  12.1 us
    all_to_all x1, starting transfers between devices, per_device(): lax.all_to_all(lax.all_to_all(fourier, 'mem', split_axis=0, concat_axis=1...  6.53 us
    convert_element_type x1, local copies, waits for them, and re-layouts, basis_table(): stacked.reshape(2 * wavenumber.shape[0], lon_count).astype(jnp.bfloat16)  6.47 us
    all_to_all x1, local copies, waits for them, and re-layouts, per_device(): lax.all_to_all(lax.all_to_all(fourier, 'mem', split_axis=0, concat_axis=1...  5.18 us
    all_to_all x1, starting transfers between devices, per_device(): lax.all_to_all(fourier, 'mem', split_axis=0, concat_axis=1, tiled=True)  4.59 us
    another operation x1, local copies, waits for them, and re-layouts, basis_table(): stacked = jnp.stack([jnp.cos(angles), -jnp.sin(angles)], axis=1)  4.19 us
  transfers between devices with their start and end apart: 3, of which 1 were waited for; matrix products, arithmetic and copies ran while one was open for 19% of the time, Pallas kernels for 0%

commit v1 on v0

--- a/solution.py
+++ b/solution.py
@@ -27,7 +27,9 @@
     )
     new_state = kept_mask[None, None, :, None, :] * updated
     coefficients = jnp.sum(new_state, axis=0).astype(jnp.bfloat16)
-    everyone = lax.all_gather(coefficients, "mem", axis=0, tiled=True)
+    everyone = jnp.concatenate(
+        lax.all_to_all(jnp.stack([coefficients] * lax.axis_size("mem")), "mem", 0, 0), axis=0
+    )
     product = jnp.einsum("bmcn,mnl->blmc", everyone, tables, preferred_element_type=jnp.float32)
     fourier = product.astype(jnp.bfloat16)
     banded = lax.all_to_all(

time: 132 us -> 153 us (1.16)
  blocking collectives: 0 us -> 71.9 us
  waiting for transfers between devices: 44.4 us -> 0.01 us
  between operations: 14.1 us -> 0.74 us
  local copies, waits for them, and re-layouts: 35.5 us -> 44 us
    all_to_all x0 -> x1, blocking collectives: none -> 71.9 us  [per_device(): lax.all_to_all(jnp.stack([coefficients] * lax.axis_size('mem')), 'mem', 0...]
    all_gather x1 -> x0, waiting for transfers between devices: 44.4 us -> none  [per_device(): everyone = lax.all_gather(coefficients, 'mem', axis=0, tiled=True)]
    reshape x0 -> x1, local copies, waits for them, and re-layouts: none -> 5.32 us  [per_device(): jnp.concatenate(lax.all_to_all(jnp.stack([coefficients] * lax.axis_size('...]
    all_to_all x0 -> x1, local copies, waits for them, and re-layouts: none -> 2.76 us  [per_device(): lax.all_to_all(jnp.stack([coefficients] * lax.axis_size('mem')), 'mem', 0...]
  transfers between devices with their start and end apart: 3 -> 2, of which waited for: 1 -> 0; matrix products, arithmetic and copies ran while one was open for 19% -> 16% of each run, Pallas kernels for 0% -> 0%
where the time goes in v1:
time: 153 us
  blocking collectives  71.9 us (47%)
  local copies, waits for them, and re-layouts  44 us (29%)
  other arithmetic  19.9 us (13%)
  starting transfers between devices  10.2 us (7%)
  matrix products  5.99 us (4%)
    all_to_all x1, blocking collectives, per_device(): lax.all_to_all(jnp.stack([coefficients] * lax.axis_size('mem')), 'mem', 0...  71.9 us
    unnamed x8, local copies, waits for them, and re-layouts  12.8 us
    another operation x1, other arithmetic  12.1 us
    all_to_all x1, starting transfers between devices, per_device(): lax.all_to_all(lax.all_to_all(fourier, 'mem', split_axis=0, concat_axis=1...  6.76 us
    convert_element_type x1, local copies, waits for them, and re-layouts, basis_table(): stacked.reshape(2 * wavenumber.shape[0], lon_count).astype(jnp.bfloat16)  6.49 us
    reshape x1, local copies, waits for them, and re-layouts, per_device(): jnp.concatenate(lax.all_to_all(jnp.stack([coefficients] * lax.axis_size('...  5.32 us
    all_to_all x1, local copies, waits for them, and re-layouts, per_device(): lax.all_to_all(lax.all_to_all(fourier, 'mem', split_axis=0, concat_axis=1...  5.18 us
    another operation x1, local copies, waits for them, and re-layouts, basis_table(): stacked = jnp.stack([jnp.cos(angles), -jnp.sin(angles)], axis=1)  4.19 us
  transfers between devices with their start and end apart: 2, of which 0 were waited for; matrix products, arithmetic and copies ran while one was open for 16% of the time, Pallas kernels for 0%

profile of v1, /device:TPU:1, one launch (start us, length us, event | category | flops | bytes accessed | tf_op | source)
XLA Modules:
  0.0 152.7 jit_solution(5764345547599936087)
XLA Ops:
  0.6 0.0 copy-start
  0.6 0.9 dynamic_slice.3
  1.5 0.1 fusion.15
  1.6 3.5 %fusion.16 = (bf16[4,8,2,1280]{3,2,1,0:T(2,128)(2,1)S(1)}, f32[3,4,8,2,1280]{4,3,2,1,0:T(2,128)}) fusion(f32[3,4,8,2,1280]{4,3,2,1,0:T(2,128)} %param.8, f32[3,1280]{1,0:T(4,128)} %param.10, f32[3,4,8,2,1280]{4,3,2,1,0:T(2,128)} %param.7, f32[3]{0:T(128)} %param.9, f32[8,1280]{1,0:T(8,128)S(1)} %fusion.15), kind=kLoop, calls=%fused_computation.22 | loop fusion | flops 1146880 | bytes 3169292 | tf_op jit(solution)/shard_map/reduce_sum | solution.py:29
  5.0 0.1 copy.23
  5.1 1.0 stack.5
  6.1 71.9 %all_to_all.38 = bf16[16,4,8,2,1280]{4,1,3,2,0:T(4,128)(2,1)S(1)} all-to-all(bf16[16,4,8,2,1280]{4,1,3,2,0:T(4,128)(2,1)S(1)} %stack.5), channel_id=1, replica_groups=mesh['mem'=16,'ma'=16] {'mem'}, dimensions={0} | all-to-all | bytes 5242880 | tf_op jit(solution)/shard_map/all_to_all | solution.py:31
  78.0 2.8 %copy.24 = bf16[16,4,8,2,1280]{4,1,0,3,2:T(4,128)(2,1)} copy(bf16[16,4,8,2,1280]{4,1,3,2,0:T(4,128)(2,1)S(1)} %all_to_all.38) | data formatting | bytes 5242880 | tf_op jit(solution)/shard_map/all_to_all | solution.py:31
  80.8 5.3 %reshape.117 = bf16[64,8,2,1280]{3,0,2,1:T(8,128)(2,1)} reshape(bf16[16,4,8,2,1280]{4,1,0,3,2:T(4,128)(2,1)} %copy.24) | data formatting | bytes 5242880 | tf_op jit(solution)/shard_map/reshape | solution.py:30
  86.1 0.0 copy-done
  86.1 0.0 copy-start.2
  86.1 2.6 %fusion.12 = bf16[64,80,8,2]{1,0,3,2:T(8,128)(2,1)S(1)} fusion(bf16[64,8,2,1280]{3,0,2,1:T(8,128)(2,1)} %reshape.117, bf16[8,1280,80]{1,2,0:T(8,128)(2,1)S(1)} %copy-done), kind=kOutput, calls=%fused_computation.17 | convolution fusion | flops 209797120 | bytes 4423680 | tf_op jit(solution)/shard_map/bmcn,mnl->blmc/dot_general | solution.py:33
  88.7 1.0 copy.25
  89.7 3.4 %all-to-all-start.1 = ((bf16[64,80,8,2]{1,3,2,0:T(2,128)(2,1)}), bf16[64,80,8,2]{1,3,2,0:T(2,128)(2,1)S(1)}, u32[]{:S(2)}, u32[]{:S(2)}) async-start(bf16[64,80,8,2]{1,3,2,0:T(2,128)(2,1)} %copy.25), calls=%async_computation.1 | async-start | bytes 524288 | tf_op jit(solution)/shard_map/all_to_all | solution.py:36
  93.1 0.0 copy-done.2
  93.1 12.1 %cosine_convert_fusion = (bf16[128,1,5120]{2,0,1:T(8,128)(2,1)S(1)}, bf16[128,1,5120]{2,0,1:T(8,128)(2,1)}) fusion(s32[128]{0:T(128)S(1)} %copy-done.2), kind=kLoop, calls=%fused_computation.9 | loop fusion | flops 7864320 | bytes 2621952 | tf_op jit(solution)/shard_map/convert
  105.2 0.0 all-to-all-done.1
  105.2 0.2 copy.33
  105.4 4.0 %copy.31 = bf16[4,16,80,8,2]{3,4,0,2,1:T(2,128)(2,1)} copy(bf16[4,16,80,8,2]{2,1,3,4,0:T(8,128)(2,1)S(1)} %bitcast.33) | data formatting | bytes 327680 | tf_op jit(solution)/shard_map/all_to_all | solution.py:36
  109.4 8.6 %reshape.120 = bf16[16,2,2560]{2,1,0:T(2,128)(2,1)} reshape(bf16[1280,4,2,8]{3,2,1,0:T(2,128)(2,1)} %bitcast.29) | data formatting | bytes 327680
  118.0 6.8 %all-to-all-start.2 = ((bf16[16,2,2560]{2,1,0:T(2,128)(2,1)}), bf16[16,2,2560]{2,1,0:T(2,128)(2,1)S(1)}, u32[]{:S(2)}, u32[]{:S(2)}) async-start(bf16[16,2,2560]{2,1,0:T(2,128)(2,1)} %reshape.120), calls=%async_computation.2 | async-start | bytes 327680 | tf_op jit(solution)/shard_map/all_to_all | solution.py:35
  124.8 1.6 %pad_maximum_fusion = bf16[128,2,5120]{2,0,1:T(8,128)(2,1)S(1)} fusion(bf16[128,1,5120]{2,0,1:T(8,128)(2,1)} %get-tuple-element.5, bf16[128,1,5120]{2,0,1:T(8,128)(2,1)S(1)} %get-tuple-element.4), kind=kLoop, calls=%fused_computation.7 | loop fusion | flops 1310720 | bytes 5242880 | tf_op jit(solution)/shard_map/stack | solution.py:14
  126.3 4.2 %copy.29 = bf16[128,2,5120]{2,1,0:T(2,128)(2,1)} copy(bf16[128,2,5120]{2,0,1:T(8,128)(2,1)S(1)} %pad_maximum_fusion) | data formatting | bytes 5242880 | tf_op jit(solution)/shard_map/stack | solution.py:14
  130.5 6.5 %convert_element_type.54 = bf16[256,5120]{1,0:T(8,128)(2,1)} reshape(bf16[128,2,5120]{2,1,0:T(2,128)(2,1)} %copy.29) | data formatting | bytes 5242880 | tf_op jit(solution)/shard_map/convert_element_type | solution.py:15
  137.0 0.0 all-to-all-done.2
  137.0 4.1 %reshape.121 = bf16[1280,4,2,8]{3,2,1,0:T(2,128)(2,1)} reshape(bf16[16,2,2560]{2,1,0:T(2,128)(2,1)S(1)} %all-to-all-done.2) | data formatting | bytes 327680
  141.1 5.2 %copy.28 = bf16[4,16,80,8,2]{2,0,4,3,1:T(4,128)(2,1)S(1)} copy(bf16[4,16,80,8,2]{3,4,0,2,1:T(2,128)(2,1)} %bitcast.30) | data formatting | bytes 327680 | tf_op jit(solution)/shard_map/all_to_all | solution.py:35
  146.3 0.2 reshape.118
  146.5 0.0 copy-start.1
  146.5 3.4 %fusion.1 = f32[320,5120]{1,0:T(8,128)S(1)} fusion(bf16[320,256]{0,1:T(8,128)(2,1)S(1)} %reshape.118, bf16[256,5120]{1,0:T(8,128)(2,1)} %convert_element_type.54), kind=kOutput, calls=%fused_computation.2 | convolution fusion | flops 843776000 | bytes 9338880 | tf_op jit(solution)/shard_map/dot_general | solution.py:45
  150.0 0.0 copy-done.1
  150.0 2.7 %multiply_convert_fusion = bf16[4,80,5120]{2,1,0:T(8,128)(2,1)} fusion(f32[4,80,5120]{2,1,0:T(8,128)S(1)} %bitcast.28, bf16[4,80,5120]{2,1,0:T(8,128)(2,1)S(1)} %copy-done.1), kind=kLoop, calls=%fused_computation.3 | loop fusion | flops 4915200 | bytes 13107200 | tf_op jit(solution)/shard_map/convert_element_type | solution.py:49
Async XLA Ops:
  0.6 85.5 %copy-start = (bf16[8,1280,80]{1,2,0:T(8,128)(2,1)S(1)}, bf16[8,1280,80]{1,2,0:T(8,128)(2,1)}, u32[]{:S(2)}) copy-start(bf16[8,1280,80]{1,2,0:T(8,128)(2,1)} %param.12) | copy-start | bytes 4915204
  86.1 7.0 %copy-start.2 = (s32[128]{0:T(128)S(1)}, s32[128]{0:T(128)}, u32[]{:S(2)}) copy-start(s32[128]{0:T(128)} %param.11) | copy-start | bytes 1540
  89.7 15.5 %all-to-all-start.1 = ((bf16[64,80,8,2]{1,3,2,0:T(2,128)(2,1)}), bf16[64,80,8,2]{1,3,2,0:T(2,128)(2,1)S(1)}, u32[]{:S(2)}, u32[]{:S(2)}) async-start(bf16[64,80,8,2]{1,3,2,0:T(2,128)(2,1)} %copy.25), calls=%async_computation.1 | async-start | bytes 524288 | tf_op jit(solution)/shard_map/all_to_all | solution.py:36
  118.0 19.0 %all-to-all-start.2 = ((bf16[16,2,2560]{2,1,0:T(2,128)(2,1)}), bf16[16,2,2560]{2,1,0:T(2,128)(2,1)S(1)}, u32[]{:S(2)}, u32[]{:S(2)}) async-start(bf16[16,2,2560]{2,1,0:T(2,128)(2,1)} %reshape.120), calls=%async_computation.2 | async-start | bytes 327680 | tf_op jit(solution)/shard_map/all_to_all | solution.py:35
  146.5 3.4 %copy-start.1 = (bf16[4,80,5120]{2,1,0:T(8,128)(2,1)S(1)}, bf16[4,80,5120]{2,1,0:T(8,128)(2,1)}, u32[]{:S(2)}) copy-start(bf16[4,80,5120]{2,1,0:T(8,128)(2,1)} %param.13) | copy-start | bytes 9830404
